TPU v7x, 32 devices: a whole 2x2x4 slice. The times are simulated.
32 devices in a mesh: dp: 8 (over z, x), expert: 4 (over y, core).
Axes of the slice: x: 2, y: 2, z: 4, core: 2. Of those that a mesh axis runs over, the one named last changes fastest.
Arguments:
- queries: bfloat16 [256, 2048], P(('dp', 'expert')), may hold values from -8 to 8
- fresh_key: bfloat16 [256, 256], P(('dp', 'expert')), may hold values from -4 to 4
- fresh_value: bfloat16 [256, 256], P(('dp', 'expert')), may hold values from -4 to 4
- cached_keys: bfloat16 [256, 128, 256], P(('dp', 'expert')), may hold values from -8 to 8
- cached_values: bfloat16 [256, 128, 256], P(('dp', 'expert')), may hold values from -4 to 4
- lengths: int32 [256], P(('dp', 'expert')), may hold values from 2 to 128
- sink_logit_rows: float32 [32], replicated, may hold values from 1 to 5
- residual: bfloat16 [256, 2880], P('dp', 'expert'), may hold values from -6 to 6
- o_weight: bfloat16 [2880, 2048], P('expert'), may hold values from -0.125 to 0.125
- norm_gain: float32 [2880], replicated, may hold values from 0.5 to 1.5
- expert_ids: int32 [256, 4], replicated, may hold values from 0 to 7, all different within a row; in each aligned block of 32 rows (0 to 31, 32 to 63, ...) at most 32 rows name the same one
- route_weights: float32 [256, 4], replicated, may hold values from 0.1 to 0.6
- w_gate_up: bfloat16 [8, 2, 2880, 2880], P('dp', None, 'expert'), may hold values from -0.109375 to 0.109375
- w_down: bfloat16 [8, 2880, 2880], P('dp', 'expert'), may hold values from -0.15625 to 0.15625
Outputs:
- layer_out: bfloat16 [256, 2880], P('dp', 'expert')
Inputs may be any that keep to these rules, and one draw needn't show every extreme that they name: `expert_ids`: each row names 4 different experts; among any aligned block of 32 rows no expert is named by more than 32 rows.
All inputs are finite; a program needn't handle non-finite values.
Results may differ from a plain program's by a relative error of at most 0.018.
Values may be sent and summed in bfloat16 or wider, within the bound.
No kernel may reach another device: no remote copies, remote signals or barrier semaphores. Data moves between devices by JAX's collectives and lax.ppermute only.
A program may use at most 64 MiB of HBM per device.

v0:
```python
import math
import jax
import jax.numpy as jnp
from jax import lax
from jax.sharding import PartitionSpec as P

D = 2880
QUERY_HEADS = 32
KEY_VALUE_HEADS = 4
HEAD_SIZE = 64
WINDOW_LENGTH = 128
TOP = 4
norm_eps = 1e-05
swish_alpha = 1.702


def attend(queries, fresh_key, fresh_value, cached_keys, cached_values, lengths, sink_logit_rows):
    batch_count = queries.shape[0]
    head_groups = QUERY_HEADS // KEY_VALUE_HEADS
    query_head_rows = queries.reshape(batch_count, KEY_VALUE_HEADS, head_groups, HEAD_SIZE)
    key_rows = cached_keys.reshape(batch_count, WINDOW_LENGTH, KEY_VALUE_HEADS, HEAD_SIZE)
    value_rows = cached_values.reshape(batch_count, WINDOW_LENGTH, KEY_VALUE_HEADS, HEAD_SIZE)
    score_scale = 1.0 / math.sqrt(HEAD_SIZE)
    cache_scores = (
        jnp.einsum("bkgd,bwkd->bkgw", query_head_rows, key_rows, preferred_element_type=jnp.float32)
        * score_scale
    )
    own_scores = (
        jnp.einsum(
            "npwm,npm->npw",
            query_head_rows,
            fresh_key.reshape(batch_count, KEY_VALUE_HEADS, HEAD_SIZE),
            preferred_element_type=jnp.float32,
        )
        * score_scale
    )
    slots = jnp.arange(WINDOW_LENGTH, dtype=jnp.int32)
    valid = (slots[None, :] >= (WINDOW_LENGTH - lengths)[:, None])[:, None, None, :]
    sink_terms = sink_logit_rows.reshape(KEY_VALUE_HEADS, head_groups)[None]
    masked = jnp.where(valid, cache_scores, -jnp.inf)
    top = jnp.maximum(jnp.maximum(jnp.max(masked, axis=-1), own_scores), sink_terms)
    cache_exp = jnp.where(valid, jnp.exp(masked - top[..., None]), 0.0)
    self_exp = jnp.exp(own_scores - top)
    total = jnp.sum(cache_exp, axis=-1) + self_exp + jnp.exp(sink_terms - top)
    cache_prob = (cache_exp / total[..., None]).astype(jnp.bfloat16)
    own_probability = (self_exp / total).astype(jnp.bfloat16)
    blended = jnp.einsum(
        "bkgw,bwkd->bkgd", cache_prob, value_rows, preferred_element_type=jnp.float32
    )
    blended = blended + own_probability.astype(jnp.float32)[..., None] * fresh_value.reshape(
        batch_count, KEY_VALUE_HEADS, 1, HEAD_SIZE
    ).astype(jnp.float32)
    return blended.reshape(batch_count, QUERY_HEADS * HEAD_SIZE).astype(jnp.bfloat16)


def slot_onehot(named, capacity):
    counts = jnp.cumsum(named.astype(jnp.int32), axis=1) - 1
    places = jnp.arange(capacity, dtype=jnp.int32)
    return named[:, None, :] & (counts[:, None, :] == places[None, :, None])


def receiver_slots(expert_ids, route_weights, expert, blocks, capacity):
    picked = expert_ids == expert
    named = jnp.any(picked, axis=1).reshape(blocks, -1)
    weight_at = jnp.sum(jnp.where(picked, route_weights, 0.0), axis=1).reshape(blocks, -1)
    onehot = slot_onehot(named, capacity)
    slot_weight = jnp.sum(jnp.where(onehot, weight_at[:, None, :], 0.0), axis=2)
    return (onehot, slot_weight)


def sender_slots(my_ids, experts, capacity):
    labels = jnp.arange(experts, dtype=jnp.int32)
    named = jnp.any(my_ids[None, :, :] == labels[:, None, None], axis=2)
    return slot_onehot(named, capacity)


def body(
    queries,
    fresh_key,
    fresh_value,
    cached_keys,
    cached_values,
    lengths,
    sink_logit_rows,
    residual,
    o_weight,
    norm_gain,
    expert_ids,
    route_weights,
    w_gate_up,
    w_down,
):
    attended = attend(
        queries, fresh_key, fresh_value, cached_keys, cached_values, lengths, sink_logit_rows
    )
    projected = lax.dot_general(
        lax.all_gather(attended, "expert", axis=0, tiled=True),
        o_weight,
        (((1,), (1,)), ((), ())),
        preferred_element_type=jnp.float32,
    )
    stream = (residual.astype(jnp.float32) + projected).astype(jnp.bfloat16)
    wide = stream.astype(jnp.float32)
    group_rows = stream.shape[0]
    columns = stream.shape[1]
    experts = lax.axis_size("dp")
    capacity = 2 * group_rows * TOP // experts
    gain_cols = lax.dynamic_slice_in_dim(norm_gain, lax.axis_index("expert") * columns, columns)
    squares = lax.psum(jnp.sum(wide * wide, axis=1), "expert")
    score_scale = lax.rsqrt(squares / D + norm_eps)
    outgoing = (wide * score_scale[:, None] * gain_cols[None, :]).astype(jnp.bfloat16)
    onehot_in, slot_weight = receiver_slots(
        expert_ids, route_weights, lax.axis_index("dp"), experts, capacity
    )
    my_ids = lax.dynamic_slice_in_dim(expert_ids, lax.axis_index("dp") * group_rows, group_rows, 0)
    onehot_out = sender_slots(my_ids, experts, capacity)
    outbound = jnp.einsum(
        "ect,td->ecd", onehot_out.astype(jnp.bfloat16), outgoing, preferred_element_type=jnp.float32
    ).astype(jnp.bfloat16)
    received = lax.all_to_all(outbound, "dp", split_axis=0, concat_axis=0, tiled=True)
    rows = received.reshape(experts * capacity, columns)
    gate_up = w_gate_up[0]
    down = w_down[0]
    both = jnp.einsum(
        "rc,hfc->rhf",
        lax.all_gather(rows, "expert", axis=1, tiled=True),
        gate_up,
        preferred_element_type=jnp.float32,
    )
    gate = both[:, 0]
    up = both[:, 1]
    hidden = ((up + 1.0) * gate * jax.nn.sigmoid(swish_alpha * gate)).astype(jnp.bfloat16)
    summed = lax.psum_scatter(
        lax.dot_general(
            down, hidden, (((0,), (1,)), ((), ())), preferred_element_type=jnp.float32
        ).astype(jnp.bfloat16),
        "expert",
        scatter_dimension=0,
        tiled=True,
    ).astype(jnp.float32)
    contribution = (summed * slot_weight.reshape(1, -1)).astype(jnp.bfloat16)
    contribution = contribution.T.reshape(experts, capacity, columns)
    returned = lax.all_to_all(contribution, "dp", split_axis=0, concat_axis=0, tiled=True)
    returned_sum = jnp.einsum(
        "ect,ecd->td",
        onehot_out.astype(jnp.float32),
        returned.astype(jnp.float32),
        precision=lax.Precision.HIGHEST,
    )
    return (wide + returned_sum).astype(jnp.bfloat16)


def solution(mesh):
    placed = (
        P(("dp", "expert"), None),
        P(("dp", "expert"), None),
        P(("dp", "expert"), None),
        P(("dp", "expert"), None, None),
        P(("dp", "expert"), None, None),
        P(("dp", "expert")),
        P(),
        P("dp", "expert"),
        P("expert", None),
        P(),
        P(),
        P(),
        P("dp", None, "expert", None),
        P("dp", "expert", None),
    )
    return jax.shard_map(
        body, mesh=mesh, in_specs=placed, out_specs=P("dp", "expert"), check_vma=False
    )
```

profile of v0, /device:TPU:0, one launch (start us, length us, event | category | flops | bytes accessed | tf_op | source)
XLA Modules:
  0.0 138.2 jit_solution(12964307490870638373)
XLA Ops:
  6.5 0.8 broadcast_subtract_fusion
  7.4 0.9 reshape.81
  8.4 1.3 copy.27
  9.7 1.4 reshape.94
  11.1 0.7 max.14
  11.8 0.9 fusion.48
  12.7 0.3 fusion.47
  13.0 0.2 fusion.28
  13.2 0.4 copy-done.1
  13.6 0.6 fusion.42
  14.3 1.3 copy.28
  15.6 0.7 reshape.87
  16.3 1.4 %fusion.12 = bf16[8,4,8,64]{3,2,1,0:T(8,128)(2,1)S(1)} fusion(bf16[8,128,4,64]{1,3,2,0:T(8,128)(2,1)S(1)} %bitcast.48, f32[8,4,8,128]{3,2,1,0:T(8,128)} %copy-done.1, f32[8,4,64]{2,1,0:T(4,128)} %reshape.87, f32[8,4,8]{2,1,0:T(4,128)} %get-tuple-element.7, f32[8,4,8]{2,1,0:T(4,128)} %get-tuple-element.8, f32[8,4,8]{2,1,0:T(4,128)S(1)} %maximum_maximum_fusion, ...), kind=kOutput, calls=%fused_computation.11 | convolution fusion | flops 4374528 | bytes 700416 | tf_op jit(solution)/shard_map/bkgw,bwkd->bkgd/dot_general | solution.py:47
  17.7 0.1 convert_element_type.86
  17.8 6.5 %all_gather.6 = bf16[32,2048]{1,0:T(8,128)(2,1)S(1)} all-gather(bf16[8,2048]{1,0:T(8,128)(2,1)S(1)} %convert_element_type.86), channel_id=1, replica_groups=mesh['dp'=8,'expert'=4] {'expert'}, dimensions={0}, use_global_device_ids=true | all-gather | bytes 163840 | tf_op jit(solution)/shard_map/all_gather | solution.py:97
  24.4 1.9 %multiply_reduce_fusion = (f32[32]{0:T(128)S(1)}, f32[32,720]{1,0:T(8,128)S(1)}) fusion(bf16[32,2048]{1,0:T(8,128)(2,1)S(1)} %all_gather.6, bf16[720,2048]{1,0:T(8,128)(2,1)S(1)} %copy-done, bf16[32,720]{1,0:T(8,128)(2,1)} %param.21), kind=kOutput, calls=%fused_computation.35 | convolution fusion | flops 94510048 | bytes 3218560 | tf_op jit(solution)/shard_map/dot_general | solution.py:96
  26.2 7.5 %psum.7 = f32[32]{0:T(128)S(1)} all-reduce(f32[32]{0:T(128)S(1)} %get-tuple-element.11), channel_id=1, replica_groups=mesh['dp'=8,'expert'=4] {'expert'}, use_global_device_ids=true, to_apply=%region_5.6 | all-reduce | flops 32 | bytes 256 | tf_op jit(solution)/shard_map/psum | solution.py:109
  33.7 0.8 constant_dynamic-slice_fusion
  34.5 0.2 reduce_window_sum.17
  34.7 0.8 dynamic_slice.7
  35.4 0.4 convolution_convert_fusion
  35.8 16.2 %all_to_all.10 = bf16[8,32,720]{2,1,0:T(8,128)(2,1)S(1)} all-to-all(bf16[8,32,720]{2,1,0:T(8,128)(2,1)S(1)} %convolution_convert_fusion), channel_id=1, replica_groups=mesh['dp'=8,'expert'=4] {'dp'}, dimensions={0} | all-to-all | bytes 737280 | tf_op jit(solution)/shard_map/all_to_all | solution.py:120
  52.1 0.9 copy.30
  53.1 17.9 %all-gather.2.cloned.1.call-done = bf16[256,2880]{0,1:T(8,128)(2,1)} async-done(((bf16[256,720]{0,1:T(8,128)(2,1)}), bf16[256,2880]{0,1:T(8,128)(2,1)}) %all-gather.2.cloned.1.call-update) | async-done | bytes 1474576 | tf_op jit(solution)/shard_map/all_gather | solution.py:126
  71.0 6.3 %fusion = f32[256,2,720]{0,2,1:T(8,128)S(1)} fusion(bf16[1,2,720,2880]{3,2,1,0:T(8,128)(2,1)} %param.26, bf16[256,2880]{0,1:T(8,128)(2,1)} %all-gather.2.cloned.1.call-done), kind=kOutput, calls=%fused_computation | convolution fusion | flops 2123366400 | bytes 11243520 | tf_op jit(solution)/shard_map/rc,hfc->rhf/dot_general | solution.py:124
  77.3 5.3 %fusion.7 = bf16[2880,256]{1,0:T(8,128)(2,1)} fusion(bf16[1,720,2880]{2,1,0:T(8,128)(2,1)} %param.27, f32[256,2,720]{0,2,1:T(8,128)S(1)} %fusion), kind=kOutput, calls=%fused_computation.5 | convolution fusion | flops 1063895040 | bytes 7096320 | tf_op jit(solution)/shard_map/dot_general | solution.py:134
  82.7 0.2 reduce_window_sum.18
  83.2 27.0 %reduce-scatter.2.cloned.1.call-done = bf16[720,256]{1,0:T(8,128)(2,1)} async-done(((bf16[2880,256]{1,0:T(8,128)(2,1)}), bf16[720,256]{1,0:T(8,128)(2,1)}) %reduce-scatter.2.cloned.1.call-update) | async-done | bytes 368656 | tf_op jit(solution)/shard_map/reduce_scatter | solution.py:133
  110.2 1.8 %fusion.20 = bf16[256,720]{0,1:T(8,128)(2,1)} fusion(bf16[720,256]{1,0:T(8,128)(2,1)} %reduce-scatter.2.cloned.1.call-done, f32[256]{0:T(256)S(1)} %mul.93), kind=kLoop, calls=%fused_computation.23 | loop fusion | flops 552960 | bytes 738304 | tf_op jit(solution)/shard_map/transpose | solution.py:142
  112.0 1.2 copy.31
  113.2 17.2 %all_to_all.11 = bf16[8,32,720]{2,1,0:T(8,128)(2,1)S(1)} all-to-all(bf16[8,32,720]{2,1,0:T(8,128)(2,1)S(1)} %bitcast.47), channel_id=1, replica_groups=mesh['dp'=8,'expert'=4] {'dp'}, dimensions={0} | all-to-all | bytes 737280 | tf_op jit(solution)/shard_map/all_to_all | solution.py:143
  130.4 1.0 fusion.16
  (29 shorter events, 0.6 us)
Async XLA Ops:
  6.5 17.8 %copy-start = (bf16[720,2048]{1,0:T(8,128)(2,1)S(1)}, bf16[720,2048]{1,0:T(8,128)(2,1)}, u32[]{:S(2)}) copy-start(bf16[720,2048]{1,0:T(8,128)(2,1)} %param.22) | copy-start | bytes 8847364
  6.5 9.1 %copy-start.4 = (bf16[8,256]{1,0:T(8,128)(2,1)S(1)}, bf16[8,256]{1,0:T(8,128)(2,1)}, u32[]{:S(2)}) copy-start(bf16[8,256]{1,0:T(8,128)(2,1)} %param.16) | copy-start | bytes 12292
  6.5 64.4 %all-gather.2.cloned.1.call-start = ((), (), s32[]{:S(2)}) async-start(), calls=%async_computation.3 | async-start | bytes 1843200 | tf_op jit(solution)/shard_map/all_gather | solution.py:126
  7.4 8.9 %copy-start.3 = (pred[8,128]{1,0:T(8,128)(4,1)}, pred[8,128]{1,0:T(8,128)(4,1)S(1)}, u32[]{:S(2)}) copy-start(pred[8,128]{1,0:T(8,128)(4,1)S(1)} %iota_compare_fusion.3) | copy-start | bytes 3076
  13.0 0.6 copy-start.1
  53.0 57.2 %reduce-scatter.2.cloned.1.call-start = ((), (), s32[]{:S(2)}) async-start(), calls=%async_computation.4 | async-start | bytes 1843200 | tf_op jit(solution)/shard_map/reduce_scatter | solution.py:133
  77.3 5.3 %copy-start.2 = (s32[256,4]{0,1:T(4,128)S(1)}, s32[256,4]{0,1:T(4,128)}, u32[]{:S(2)}) copy-start(s32[256,4]{0,1:T(4,128)} %param.24) | copy-start | bytes 12292
  77.3 5.6 %copy-start.5 = (f32[256,4]{0,1:T(4,128)S(1)}, f32[256,4]{0,1:T(4,128)}, u32[]{:S(2)}) copy-start(f32[256,4]{0,1:T(4,128)} %param.25) | copy-start | bytes 12292
Sparse Core Ops, SparseCore 0:
  53.1 17.7 all-gather.1
  82.7 27.4 reduce-scatter.1
where the time goes:
time: 139 us; the launch traced here: 138 us
  blocking collectives  47.5 us (34%)
  waiting for transfers between devices  44.9 us (32%)
  matrix products  17.4 us (13%)
  between operations  13.5 us (10%)
  local copies, waits for them, and re-layouts  10.8 us (8%)
  other arithmetic  4.1 us (3%)
    reduce_scatter x1, waiting for transfers between devices, body(): lax.psum_scatter(lax.dot_general(down, hidden, (((0,), (1,)), ((), ())),...  27 us
    all_gather x1, waiting for transfers between devices, body(): lax.all_gather(rows, 'expert', axis=1, tiled=True)  17.9 us
    all_to_all x1, blocking collectives, body(): lax.all_to_all(contribution, 'dp', split_axis=0, concat_axis=0, tiled=True)  17.2 us
    all_to_all x1, blocking collectives, body(): lax.all_to_all(outbound, 'dp', split_axis=0, concat_axis=0, tiled=True)  16.2 us
    psum x1, blocking collectives, body(): squares = lax.psum(jnp.sum(wide * wide, axis=1), 'expert')  7.47 us
    all_gather x1, blocking collectives, body(): lax.all_gather(attended, 'expert', axis=0, tiled=True)  6.54 us
    dot_general x1, matrix products, body(): jnp.einsum('rc,hfc->rhf', lax.all_gather(rows, 'expert', axis=1, tiled=Tr...  6.32 us
    dot_general x1, matrix products, body(): lax.dot_general(down, hidden, (((0,), (1,)), ((), ())), preferred_element...  5.28 us
  transfers between devices with their start and end apart: 2, of which 2 were waited for; matrix products, arithmetic and copies ran while one was open for 0% of the time, Pallas kernels for 0%

commit v1 on v0

--- a/solution.py
+++ b/solution.py
@@ -12,6 +12,28 @@
 TOP = 4
 norm_eps = 1e-05
 swish_alpha = 1.702
+
+
+def hold_figure(view, vector):
+    named_axis = "expert"
+    extra = jax.lax.axis_size(named_axis)
+    inter = jax.lax.axis_index(named_axis)
+    heard, state_next = (extra, inter)
+    pages = []
+    idx = 0
+    while idx < heard:
+        pages.append((idx, (idx - 1) % heard))
+        idx += 1
+    latest = view.shape[1]
+    res = view
+    value_now = vector(res, state_next * latest)
+    tick = 1
+    while tick < heard:
+        res = jax.lax.ppermute(res, axis_name=named_axis, perm=pages)
+        step_out = vector(res, (state_next + tick) % heard * latest)
+        value_now = value_now + step_out
+        tick = tick + 1
+    return value_now
 
 
 def attend(queries, fresh_key, fresh_value, cached_keys, cached_values, lengths, sink_logit_rows):
@@ -121,11 +143,14 @@
     rows = received.reshape(experts * capacity, columns)
     gate_up = w_gate_up[0]
     down = w_down[0]
-    both = jnp.einsum(
-        "rc,hfc->rhf",
-        lax.all_gather(rows, "expert", axis=1, tiled=True),
-        gate_up,
-        preferred_element_type=jnp.float32,
+    both = hold_figure(
+        rows,
+        vector=lambda shard, offset: jnp.einsum(
+            "rc,hfc->rhf",
+            shard,
+            lax.dynamic_slice_in_dim(gate_up, offset, shard.shape[1], axis=2),
+            preferred_element_type=jnp.float32,
+        ),
     )
     gate = both[:, 0]
     up = both[:, 1]

time: 139 us -> 133 us (0.957)
  waiting for transfers between devices: 44.9 us -> 33.9 us
  starting transfers between devices: 0.04 us -> 3.82 us
  matrix products: 17.4 us -> 20.5 us
    all_gather x1 -> x0, waiting for transfers between devices: 17.9 us -> none  [body(): lax.all_gather(rows, 'expert', axis=1, tiled=True)]
    ppermute x0 -> x3, waiting for transfers between devices: none -> 7.97 us  [hold_figure(): res = jax.lax.ppermute(res, axis_name=named_axis, perm=pages)]
    dot_general x1 -> x4, matrix products: 6.32 us -> 11.5 us  [body(): jnp.einsum('rc,hfc->rhf', shard, lax.dynamic_slice_in_dim(gate_up, offset...]
    ppermute x0 -> x3, starting transfers between devices: none -> 3.82 us  [hold_figure(): res = jax.lax.ppermute(res, axis_name=named_axis, perm=pages)]
    dot_general x1, matrix products: 5.28 us -> 3.15 us  [body(): lax.dot_general(down, hidden, (((0,), (1,)), ((), ())), preferred_element...]
    unnamed x14 -> x16, local copies, waits for them, and re-layouts: 3.05 us -> 3.54 us
  transfers between devices with their start and end apart: 2 -> 4, of which waited for: 2 -> 3; matrix products, arithmetic and copies ran while one was open for 0% -> 7% of each run, Pallas kernels for 0% -> 0%
where the time goes in v1:
time: 133 us
  blocking collectives  47.5 us (36%)
  waiting for transfers between devices  33.9 us (25%)
  matrix products  20.5 us (15%)
  between operations  13.6 us (10%)
  local copies, waits for them, and re-layouts  9.87 us (7%)
  starting transfers between devices  3.82 us (3%)
  other arithmetic  3.35 us (3%)
    reduce_scatter x1, waiting for transfers between devices, body(): lax.psum_scatter(lax.dot_general(down, hidden, (((0,), (1,)), ((), ())),...  25.9 us
    all_to_all x1, blocking collectives, body(): lax.all_to_all(contribution, 'dp', split_axis=0, concat_axis=0, tiled=True)  17.2 us
    all_to_all x1, blocking collectives, body(): lax.all_to_all(outbound, 'dp', split_axis=0, concat_axis=0, tiled=True)  16.2 us
    dot_general x4, matrix products, body(): jnp.einsum('rc,hfc->rhf', shard, lax.dynamic_slice_in_dim(gate_up, offset...  11.5 us
    ppermute x3, waiting for transfers between devices, hold_figure(): res = jax.lax.ppermute(res, axis_name=named_axis, perm=pages)  7.97 us
    psum x1, blocking collectives, body(): squares = lax.psum(jnp.sum(wide * wide, axis=1), 'expert')  7.48 us
    all_gather x1, blocking collectives, body(): lax.all_gather(attended, 'expert', axis=0, tiled=True)  6.54 us
    ppermute x3, starting transfers between devices, hold_figure(): res = jax.lax.ppermute(res, axis_name=named_axis, perm=pages)  3.82 us
  transfers between devices with their start and end apart: 4, of which 3 were waited for; matrix products, arithmetic and copies ran while one was open for 7% of the time, Pallas kernels for 0%

profile of v1, /device:TPU:0, one launch (start us, length us, event | category | flops | bytes accessed | tf_op | source)
XLA Modules:
  0.0 132.5 jit_solution(8633928777382676332)
XLA Ops:
  6.6 2.2 %copy.30 = bf16[8,128,256]{1,2,0:T(8,128)(2,1)} copy(bf16[8,128,256]{2,1,0:T(8,128)(2,1)} %param.18) | data formatting | bytes 1048576 | tf_op args[4]
  8.7 0.9 reshape.85
  9.6 1.3 copy.29
  11.0 0.7 broadcast_subtract_fusion
  11.7 1.4 %reshape.91 = f32[8,4,64]{2,1,0:T(4,128)} reshape(bf16[8,256]{1,0:T(8,128)(2,1)} %param.16) | data formatting | bytes 12288 | tf_op jit(solution)/shard_map/convert_element_type | solution.py:74
  13.1 0.7 reshape.101
  13.8 0.9 fusion.66
  14.7 0.3 fusion.65
  15.1 0.2 fusion.42
  15.3 1.5 %fusion.23 = bf16[8,4,8,64]{3,2,1,0:T(8,128)(2,1)S(1)} fusion(bf16[8,128,4,64]{1,3,2,0:T(8,128)(2,1)} %bitcast.69, f32[8,4,8,128]{3,2,1,0:T(8,128)S(1)} %get-tuple-element.10, f32[8,4,64]{2,1,0:T(4,128)} %reshape.91, f32[8,4,8]{2,1,0:T(4,128)S(1)} %get-tuple-element.7, f32[8,4,8]{2,1,0:T(4,128)S(1)} %get-tuple-element.8, ...), kind=kOutput, calls=%fused_computation.21 | convolution fusion | flops 4374528 | bytes 700416 | tf_op jit(solution)/shard_map/bkgw,bwkd->bkgd/dot_general | solution.py:69
  17.0 6.5 %all_gather.3 = bf16[32,2048]{1,0:T(8,128)(2,1)S(1)} all-gather(bf16[8,2048]{1,0:T(8,128)(2,1)S(1)} %convert_element_type.86), channel_id=1, replica_groups=mesh['dp'=8,'expert'=4] {'expert'}, dimensions={0}, use_global_device_ids=true | all-gather | bytes 163840 | tf_op jit(solution)/shard_map/all_gather | solution.py:119
  23.6 0.2 reduce_window_sum.17
  23.8 1.9 %multiply_reduce_fusion = (f32[32]{0:T(128)S(1)}, f32[32,720]{1,0:T(8,128)S(1)}) fusion(bf16[32,2048]{1,0:T(8,128)(2,1)S(1)} %all_gather.3, bf16[720,2048]{1,0:T(8,128)(2,1)S(1)} %copy-done, bf16[32,720]{1,0:T(8,128)(2,1)} %param.21), kind=kOutput, calls=%fused_computation.48 | convolution fusion | flops 94510048 | bytes 3218560 | tf_op jit(solution)/shard_map/dot_general | solution.py:118
  25.6 7.5 %psum.7 = f32[32]{0:T(128)S(1)} all-reduce(f32[32]{0:T(128)S(1)} %get-tuple-element.11), channel_id=1, replica_groups=mesh['dp'=8,'expert'=4] {'expert'}, use_global_device_ids=true, to_apply=%region_5.6 | all-reduce | flops 32 | bytes 256 | tf_op jit(solution)/shard_map/psum | solution.py:131
  33.1 0.8 dynamic_slice.27
  33.9 0.4 convolution_convert_fusion
  34.3 16.2 %all_to_all.10 = bf16[8,32,720]{2,1,0:T(8,128)(2,1)S(1)} all-to-all(bf16[8,32,720]{2,1,0:T(8,128)(2,1)S(1)} %convolution_convert_fusion), channel_id=1, replica_groups=mesh['dp'=8,'expert'=4] {'dp'}, dimensions={0} | all-to-all | bytes 737280 | tf_op jit(solution)/shard_map/all_to_all | solution.py:142
  50.5 0.9 copy.33
  51.4 5.3 %collective-permute-done = bf16[256,720]{0,1:T(8,128)(2,1)} collective-permute-done((bf16[256,720]{0,1:T(8,128)(2,1)}, bf16[256,720]{0,1:T(8,128)(2,1)}, u32[]{:S(2)}, u32[]{:S(2)}) %collective-permute-start) | collective-permute-done | bytes 368672 | tf_op jit(solution)/shard_map/ppermute | solution.py:32
  56.8 1.9 %collective-permute-start.1 = (bf16[256,720]{0,1:T(8,128)(2,1)}, bf16[256,720]{0,1:T(8,128)(2,1)}, u32[]{:S(2)}, u32[]{:S(2)}) collective-permute-start(bf16[256,720]{0,1:T(8,128)(2,1)} %collective-permute-done), channel_id=1, source_target_pairs={{0,3},{1,0},{2,1},{3,2},{4,7},{5,4},{6,5},{7,6},{8,11},{9,8},{10,9... | collective-permute-start | bytes 1105928 | tf_op jit(solution)/shard_map/ppermute | solution.py:32
  58.7 2.7 %fusion.14 = f32[256,2,720]{0,2,1:T(8,128)S(1)} fusion(bf16[256,720,1]{1,0,2:T(8,128)(2,1)S(1)} %bitcast.66, bf16[1,2,720,2880]{3,2,1,0:T(8,128)(2,1)} %param.26, s32[]{:T(128)S(6)} %select_n.49), kind=kOutput, calls=%fused_computation.10 | convolution fusion | flops 530841600 | bytes 4055044 | tf_op jit(solution)/shard_map/rc,hfc->rhf/dot_general | solution.py:148
  61.4 2.6 %collective-permute-done.1 = bf16[256,720]{0,1:T(8,128)(2,1)} collective-permute-done((bf16[256,720]{0,1:T(8,128)(2,1)}, bf16[256,720]{0,1:T(8,128)(2,1)}, u32[]{:S(2)}, u32[]{:S(2)}) %collective-permute-start.1) | collective-permute-done | bytes 368672 | tf_op jit(solution)/shard_map/ppermute | solution.py:32
  64.0 1.9 %collective-permute-start.2 = (bf16[256,720]{0,1:T(8,128)(2,1)}, bf16[256,720]{0,1:T(8,128)(2,1)S(1)}, u32[]{:S(2)}, u32[]{:S(2)}) collective-permute-start(bf16[256,720]{0,1:T(8,128)(2,1)} %collective-permute-done.1), channel_id=1, source_target_pairs={{0,3},{1,0},{2,1},{3,2},{4,7},{5,4},{6,5},{7,6},{8,11},{9,8},{10,9... | collective-permute-start | bytes 1105928 | tf_op jit(solution)/shard_map/ppermute | solution.py:32
  66.0 2.9 %fusion.12 = f32[256,2,720]{0,2,1:T(8,128)S(1)} fusion(bf16[1,2,720,2880]{3,2,1,0:T(8,128)(2,1)} %param.26, s32[]{:T(128)S(6)} %select_n.51, bf16[256,720]{0,1:T(8,128)(2,1)} %collective-permute-done), kind=kOutput, calls=%fused_computation.8 | convolution fusion | flops 530841600 | bytes 4055044 | tf_op jit(solution)/shard_map/rc,hfc->rhf/dot_general | solution.py:148
  68.9 3.0 %fusion.10 = f32[256,2,720]{0,2,1:T(8,128)S(1)} fusion(bf16[1,2,720,2880]{3,2,1,0:T(8,128)(2,1)} %param.26, s32[]{:T(128)S(6)} %select_n.53, bf16[256,720]{0,1:T(8,128)(2,1)} %collective-permute-done.1), kind=kOutput, calls=%fused_computation.6 | convolution fusion | flops 530841600 | bytes 4055044 | tf_op jit(solution)/shard_map/rc,hfc->rhf/dot_general | solution.py:148
  71.9 2.8 %add_add_fusion = f32[256,2,720]{0,2,1:T(8,128)S(1)} fusion(f32[256,2,720]{0,2,1:T(8,128)S(1)} %fusion.10, f32[256,2,720]{0,2,1:T(8,128)S(1)} %fusion.14, f32[256,2,720]{0,2,1:T(8,128)S(1)} %fusion.12, bf16[1,2,720,2880]{3,2,1,0:T(8,128)(2,1)} %param.26, s32[]{:T(128)S(6)} %select_n.55, bf16[256,720]{0,1:T(8,128)(2,1)S(1)} %collective-permute-done.2), kind=kOutput, calls=%fused_computation.16 | convolution fusion | flops 531947520 | bytes 8478724 | tf_op jit(solution)/shard_map/rc,hfc->rhf/dot_general | solution.py:148
  74.8 3.2 %fusion.5 = bf16[2880,256]{1,0:T(8,128)(2,1)} fusion(bf16[1,720,2880]{2,1,0:T(8,128)(2,1)S(1)} %bitcast.73, f32[256,2,720]{0,2,1:T(8,128)S(1)} %add_add_fusion), kind=kOutput, calls=%fused_computation.3 | convolution fusion | flops 1063895040 | bytes 7096320 | tf_op jit(solution)/shard_map/dot_general | solution.py:159
  78.6 25.9 %reduce-scatter.2.cloned.1.call-done = bf16[720,256]{1,0:T(8,128)(2,1)} async-done(((bf16[2880,256]{1,0:T(8,128)(2,1)}), bf16[720,256]{1,0:T(8,128)(2,1)}) %reduce-scatter.2.cloned.1.call-update) | async-done | bytes 368656 | tf_op jit(solution)/shard_map/reduce_scatter | solution.py:158
  104.5 1.8 %fusion.31 = bf16[256,720]{0,1:T(8,128)(2,1)} fusion(bf16[720,256]{1,0:T(8,128)(2,1)} %reduce-scatter.2.cloned.1.call-done, f32[256]{0:T(256)S(1)} %mul.106), kind=kLoop, calls=%fused_computation.33 | loop fusion | flops 552960 | bytes 738304 | tf_op jit(solution)/shard_map/transpose | solution.py:167
  106.3 1.2 copy.34
  107.5 17.2 %all_to_all.11 = bf16[8,32,720]{2,1,0:T(8,128)(2,1)S(1)} all-to-all(bf16[8,32,720]{2,1,0:T(8,128)(2,1)S(1)} %bitcast.68), channel_id=1, replica_groups=mesh['dp'=8,'expert'=4] {'dp'}, dimensions={0} | all-to-all | bytes 737280 | tf_op jit(solution)/shard_map/all_to_all | solution.py:168
  124.7 1.0 fusion.27
  (38 shorter events, 1.1 us)
Async XLA Ops:
  6.5 17.3 %copy-start = (bf16[720,2048]{1,0:T(8,128)(2,1)S(1)}, bf16[720,2048]{1,0:T(8,128)(2,1)}, u32[]{:S(2)}) copy-start(bf16[720,2048]{1,0:T(8,128)(2,1)} %param.22) | copy-start | bytes 8847364
  6.5 6.5 %copy-start.2 = (bf16[8,256]{1,0:T(8,128)(2,1)S(1)}, bf16[8,256]{1,0:T(8,128)(2,1)}, u32[]{:S(2)}) copy-start(bf16[8,256]{1,0:T(8,128)(2,1)} %param.15) | copy-start | bytes 12292
  6.5 7.2 %copy-start.4 = (f32[32]{0:T(128)S(1)}, f32[32]{0:T(128)}, u32[]{:S(2)}) copy-start(f32[32]{0:T(128)} %param.20) | copy-start | bytes 388
  6.5 98.0 %reduce-scatter.2.cloned.1.call-start = ((), (), s32[]{:S(2)}) async-start(), calls=%async_computation.3 | async-start | bytes 1843200 | tf_op jit(solution)/shard_map/reduce_scatter | solution.py:158
  8.7 14.8 %copy-start.1 = (s32[256,4]{0,1:T(4,128)S(1)}, s32[256,4]{0,1:T(4,128)}, u32[]{:S(2)}) copy-start(s32[256,4]{0,1:T(4,128)} %param.24) | copy-start | bytes 12292
  51.4 5.4 %collective-permute-start = (bf16[256,720]{0,1:T(8,128)(2,1)}, bf16[256,720]{0,1:T(8,128)(2,1)}, u32[]{:S(2)}, u32[]{:S(2)}) collective-permute-start(bf16[256,720]{0,1:T(8,128)(2,1)} %copy.33), channel_id=1, source_target_pairs={{0,3},{1,0},{2,1},{3,2},{4,7},{5,4},{6,5},{7,6},{8,11},{9,8},{10,9... | collective-permute-start | bytes 1105928 | tf_op jit(solution)/shard_map/ppermute | solution.py:32
  56.8 7.3 %collective-permute-start.1 = (bf16[256,720]{0,1:T(8,128)(2,1)}, bf16[256,720]{0,1:T(8,128)(2,1)}, u32[]{:S(2)}, u32[]{:S(2)}) collective-permute-start(bf16[256,720]{0,1:T(8,128)(2,1)} %collective-permute-done), channel_id=1, source_target_pairs={{0,3},{1,0},{2,1},{3,2},{4,7},{5,4},{6,5},{7,6},{8,11},{9,8},{10,9... | collective-permute-start | bytes 1105928 | tf_op jit(solution)/shard_map/ppermute | solution.py:32
  64.0 7.8 %collective-permute-start.2 = (bf16[256,720]{0,1:T(8,128)(2,1)}, bf16[256,720]{0,1:T(8,128)(2,1)S(1)}, u32[]{:S(2)}, u32[]{:S(2)}) collective-permute-start(bf16[256,720]{0,1:T(8,128)(2,1)} %collective-permute-done.1), channel_id=1, source_target_pairs={{0,3},{1,0},{2,1},{3,2},{4,7},{5,4},{6,5},{7,6},{8,11},{9,8},{10,9... | collective-permute-start | bytes 1105928 | tf_op jit(solution)/shard_map/ppermute | solution.py:32
  68.8 5.9 %slice-start = ((s8[4239360]{0:T(1024)(128)(4,1)}), s8[4194304]{0:T(1024)(128)(4,1)S(1)}, s32[]{:S(2)}) async-start(s8[4239360]{0:T(1024)(128)(4,1)} %bitcast.72), calls=%async_computation.4 | async-start | bytes 8388608
  71.9 2.9 %slice-start.1 = ((s8[4239360]{0:T(1024)(128)(4,1)}), s8[45056]{0:T(1024)(128)(4,1)S(1)}, s32[]{:S(2)}) async-start(s8[4239360]{0:T(1024)(128)(4,1)} %bitcast.72), calls=%async_computation.5 | async-start | bytes 90112
  74.8 3.2 %copy-start.3 = (f32[256,4]{0,1:T(4,128)S(1)}, f32[256,4]{0,1:T(4,128)}, u32[]{:S(2)}) copy-start(f32[256,4]{0,1:T(4,128)} %param.25) | copy-start | bytes 12292
Sparse Core Ops, SparseCore 0:
  78.1 26.3 reduce-scatter.1
